TPU v7x, 128 devices: a whole 4x4x4 slice. The times are simulated.
128 devices in a mesh: section: 8 (over y_hi, x), seq: 16 (over z, y_lo, core).
Axes of the slice: x: 4, y: 4 (y_hi: 2, y_lo: 2; y = y_hi * 2 + y_lo), z: 4, core: 2. Of those that a mesh axis runs over, the one named last changes fastest.
Arguments:
- tokens: bfloat16 [8, 4096, 4096], P('section', 'seq'), may hold values from -6 to 6
- norm_gain: bfloat16 [8, 4096], P('section'), may hold values from 0.099609375 to 1.8984375
- w_query: bfloat16 [8, 4096, 2048], P('section', 'seq'), may hold values from -0.09375 to 0.09375
- w_key: bfloat16 [8, 4096, 512], P('section', 'seq'), may hold values from -1.903125 to 1.903125
- w_value: bfloat16 [8, 4096, 512], P('section', 'seq'), may hold values from -0.09375 to 0.09375
Outputs:
- received: bfloat16 [8, 4096, 2048], P('section', 'seq')
All inputs are finite; a program needn't handle non-finite values.
Results may differ from a plain program's by a relative error of at most 0.012.
The roundings to bfloat16 on the way count: a program that leaves them out, or rounds other values in their place, can miss the bound.
Values may be sent and summed in bfloat16 or wider, within the bound.
No kernel may reach another device: no remote copies, remote signals or barrier semaphores. Data moves between devices by JAX's collectives and lax.ppermute only.
A program may use at most 192 MiB of HBM per device.

v0:
```python
import jax
import jax.numpy as jnp
from jax import lax
from jax.sharding import PartitionSpec as P

LOCAL_QUERY_HEADS = 16
LOCAL_KEY_HEADS = 4
HEAD_SIZE = 128


def shifted(block, axis, distance):
    devices = range(lax.axis_size(axis))
    route = [((i - distance) % len(devices), i) for i in devices]
    return lax.ppermute(block, axis, route)


def normalize(rows_in, gain_row):
    wide = rows_in.astype(jnp.float32)
    scale = lax.rsqrt(jnp.mean(wide * wide, axis=-1, keepdims=True) + 1e-05)
    return (wide * scale * gain_row.astype(jnp.float32)).astype(jnp.bfloat16)


def rotate(matrix, positions):
    row_count = matrix.shape[0]
    head_count = matrix.shape[1] // HEAD_SIZE
    half_dim = HEAD_SIZE // 2
    shaped = matrix.reshape(row_count, head_count, HEAD_SIZE)
    freqs = jnp.power(
        jnp.float32(500000.0), -(jnp.arange(half_dim).astype(jnp.float32) * 2.0 / HEAD_SIZE)
    )
    angles = positions[:, None] * freqs[None, :]
    cosine = jnp.cos(angles)[:, None, :]
    sine_part = jnp.sin(angles)[:, None, :]
    first_half = shaped[:, :, :half_dim]
    second_half = shaped[:, :, half_dim:]
    turned = jnp.concatenate(
        [
            first_half * cosine - second_half * sine_part,
            second_half * cosine + first_half * sine_part,
        ],
        axis=2,
    )
    return turned.reshape(row_count, head_count * HEAD_SIZE)


def expand(matrix):
    row_count = matrix.shape[0]
    kv_count = matrix.shape[1] // HEAD_SIZE
    query_group_count = LOCAL_QUERY_HEADS // LOCAL_KEY_HEADS
    wide = jnp.broadcast_to(
        matrix.reshape(row_count, kv_count, 1, HEAD_SIZE),
        (row_count, kv_count, query_group_count, HEAD_SIZE),
    )
    return wide.reshape(row_count, kv_count * query_group_count * HEAD_SIZE)


def attend(queries, key_rows, value_rows):
    row_count = queries.shape[0]
    head_count = queries.shape[1] // HEAD_SIZE
    block_rows = min(512, row_count)
    key_heads = key_rows.reshape(row_count, head_count, HEAD_SIZE)
    value_heads = value_rows.reshape(row_count, head_count, HEAD_SIZE)
    key_places = jnp.arange(row_count)

    def one_block(block_index):
        first_row = block_index * block_rows
        query_block = lax.dynamic_slice_in_dim(queries, first_row, block_rows, 0).reshape(
            block_rows, head_count, HEAD_SIZE
        )
        scores = jnp.einsum(
            "qhd,khd->hqk", query_block, key_heads, preferred_element_type=jnp.float32
        ) / jnp.sqrt(jnp.float32(HEAD_SIZE))
        query_places = first_row + jnp.arange(block_rows)
        causal = key_places[None, :] <= query_places[:, None]
        scores = jnp.where(causal[None, :, :], scores, -jnp.inf)
        maxima = jnp.max(scores, axis=-1, keepdims=True)
        expon = jnp.exp(scores - maxima)
        probs = (expon / jnp.sum(expon, axis=-1, keepdims=True)).astype(jnp.bfloat16)
        mixed = jnp.einsum("hqk,khd->qhd", probs, value_heads, preferred_element_type=jnp.float32)
        return mixed.astype(jnp.bfloat16).reshape(block_rows, head_count * HEAD_SIZE)

    blocks = lax.map(one_block, jnp.arange(row_count // block_rows))
    return blocks.reshape(row_count, head_count * HEAD_SIZE)


def per_device(tokens, norm_gain, w_query, w_key, w_value):
    normed = normalize(tokens[0], norm_gain[0])
    local_rows = normed.shape[0]
    query_weight = w_query[0]
    key_weight = w_key[0]
    value_weight = w_value[0]
    pieces = (
        lax.all_gather(query_weight, "seq", axis=0, tiled=True),
        lax.all_gather(key_weight, "seq", axis=0, tiled=True),
        lax.all_gather(value_weight, "seq", axis=0, tiled=True),
    )
    query_raw, key_raw, value_raw = tuple(
        (jnp.dot(normed, piece, preferred_element_type=jnp.float32) for piece in pieces)
    )
    positions = (lax.axis_index("seq") * local_rows + jnp.arange(local_rows)).astype(jnp.float32)
    queries = rotate(query_raw, positions).astype(jnp.bfloat16)
    key_rows = expand(rotate(key_raw, positions).astype(jnp.bfloat16))
    value_rows = expand(value_raw.astype(jnp.bfloat16))
    head_queries, head_keys, head_values = (
        lax.all_to_all(queries, "seq", split_axis=1, concat_axis=0, tiled=True),
        lax.all_to_all(key_rows, "seq", split_axis=1, concat_axis=0, tiled=True),
        lax.all_to_all(value_rows, "seq", split_axis=1, concat_axis=0, tiled=True),
    )
    attended = attend(head_queries, head_keys, head_values)
    token_layout = lax.all_to_all(attended, "seq", split_axis=0, concat_axis=1, tiled=True)
    arrived = shifted(token_layout, "section", 1)
    return arrived[None]


def solution(mesh):
    return jax.shard_map(
        per_device,
        mesh=mesh,
        in_specs=(
            P("section", "seq", None),
            P("section", None),
            P("section", "seq", None),
            P("section", "seq", None),
            P("section", "seq", None),
        ),
        out_specs=P("section", "seq", None),
        check_vma=False,
    )
```

profile of v0, /device:TPU:0, one launch (start us, length us, event | category | flops | bytes accessed | tf_op | source)
XLA Modules:
  0.0 348.0 jit_solution(4514223311323205779)
XLA Ops:
  6.5 0.7 all-gather.9.cloned.1.call-update
  7.3 0.7 all-gather.7.cloned.1.call-update
  8.1 0.7 all-gather.11.cloned.1.call-update
  8.7 0.7 mul.157
  9.5 2.1 fusion.13
  11.6 0.3 multiply_cosine_fusion
  11.9 37.0 %all-gather.9.cloned.1.call-done = bf16[1,4096,512]{2,1,0:T(8,128)(2,1)} async-done(((bf16[1,256,512]{2,1,0:T(8,128)(2,1)}), bf16[1,4096,512]{2,1,0:T(8,128)(2,1)}) %all-gather.9.cloned.1.call-update) | async-done | bytes 4194320 | tf_op jit(solution)/shard_map/all_gather | solution.py:94
  48.9 6.5 %copy.24 = bf16[512,4096]{1,0:T(8,128)(2,1)} copy(bf16[512,4096]{0,1:T(8,128)(2,1)} %bitcast.89) | data formatting | bytes 8388608 | tf_op jit(solution)/shard_map/dot_general | solution.py:98
  55.4 3.5 %fusion.34 = f32[256,4,128]{0,2,1:T(8,128)S(1)} fusion(bf16[4,128,4096]{2,1,0:T(8,128)(2,1)} %bitcast.90, bf16[1,256,4096]{2,1,0:T(8,128)(2,1)S(1)} %copy-done, f32[4096]{0:T(1024)S(1)} %bitcast.99, f32[256]{0:T(256)S(1)} %add_rsqrt_fusion), kind=kOutput, calls=%fused_computation.34 | convolution fusion | flops 1077936128 | bytes 6833152 | tf_op jit(solution)/shard_map/dot_general | solution.py:98
  59.1 0.2 copy.25
  59.3 1.2 broadcast_in_dim.17
  60.5 4.2 %all-to-all-start.1 = ((bf16[256,16,128]{2,0,1:T(8,128)(2,1)}), bf16[256,16,128]{2,0,1:T(8,128)(2,1)S(1)}, u32[]{:S(2)}, u32[]{:S(2)}) async-start(bf16[256,16,128]{2,0,1:T(8,128)(2,1)} %bitcast.12), calls=%async_computation.1 | async-start | bytes 2097152 | tf_op jit(solution)/shard_map/all_to_all | solution.py:106
  64.6 88.7 %all-gather.7.cloned.1.call-done = bf16[1,4096,2048]{2,1,0:T(8,128)(2,1)} async-done(((bf16[1,256,2048]{2,1,0:T(8,128)(2,1)}), bf16[1,4096,2048]{2,1,0:T(8,128)(2,1)}) %all-gather.7.cloned.1.call-update) | async-done | bytes 16777232 | tf_op jit(solution)/shard_map/all_gather | solution.py:93
  153.4 20.7 %copy.22 = bf16[2048,4096]{1,0:T(8,128)(2,1)} copy(bf16[2048,4096]{0,1:T(8,128)(2,1)} %bitcast.87) | data formatting | bytes 33554432 | tf_op jit(solution)/shard_map/dot_general | solution.py:98
  174.1 8.5 %fusion.36 = f32[256,16,128]{0,2,1:T(8,128)S(1)} fusion(bf16[16,128,4096]{2,1,0:T(8,128)(2,1)} %bitcast.88, bf16[1,256,4096]{2,1,0:T(8,128)(2,1)S(1)} %copy-done, f32[4096]{0:T(1024)S(1)} %bitcast.100, f32[256]{0:T(256)S(1)} %add_rsqrt_fusion), kind=kOutput, calls=%fused_computation.35 | convolution fusion | flops 4299161600 | bytes 20988928 | tf_op jit(solution)/shard_map/dot_general | solution.py:98
  182.6 0.3 subtract_convert_fusion
  182.9 1.0 pad_maximum_fusion
  184.0 1.0 copy-done.1
  185.0 4.9 %all-to-all-start = ((bf16[256,16,128]{0,2,1:T(8,128)(2,1)}), bf16[256,16,128]{0,2,1:T(8,128)(2,1)S(1)}, u32[]{:S(2)}, u32[]{:S(2)}) async-start(bf16[256,16,128]{0,2,1:T(8,128)(2,1)} %pad_maximum_fusion), calls=%async_computation | async-start | bytes 2097152 | tf_op jit(solution)/shard_map/all_to_all | solution.py:105
  189.9 3.6 %all-gather.11.cloned.1.call-done = bf16[1,4096,512]{2,1,0:T(8,128)(2,1)} async-done(((bf16[1,256,512]{2,1,0:T(8,128)(2,1)}), bf16[1,4096,512]{2,1,0:T(8,128)(2,1)}) %all-gather.11.cloned.1.call-update) | async-done | bytes 4194320 | tf_op jit(solution)/shard_map/all_gather | solution.py:95
  193.5 3.5 fusion.29
  197.0 9.4 %all-to-all-done = bf16[256,16,128]{0,2,1:T(8,128)(2,1)S(1)} async-done(((bf16[256,16,128]{0,2,1:T(8,128)(2,1)}), bf16[256,16,128]{0,2,1:T(8,128)(2,1)S(1)}, u32[]{:S(2)}, u32[]{:S(2)}) %all-to-all-start) | async-done | bytes 1048608 | tf_op jit(solution)/shard_map/all_to_all | solution.py:105
  206.4 1.2 broadcast_in_dim.19
  207.6 3.8 %all-to-all-start.2 = ((bf16[256,16,128]{2,0,1:T(8,128)(2,1)}), bf16[256,16,128]{2,0,1:T(8,128)(2,1)S(1)}, u32[]{:S(2)}, u32[]{:S(2)}) async-start(bf16[256,16,128]{2,0,1:T(8,128)(2,1)} %bitcast.16), calls=%async_computation.2 | async-start | bytes 2097152 | tf_op jit(solution)/shard_map/all_to_all | solution.py:107
  211.4 1.3 copy.23
  212.8 15.0 %all-to-all-done.2 = bf16[256,16,128]{2,0,1:T(8,128)(2,1)S(1)} async-done(((bf16[256,16,128]{2,0,1:T(8,128)(2,1)}), bf16[256,16,128]{2,0,1:T(8,128)(2,1)S(1)}, u32[]{:S(2)}, u32[]{:S(2)}) %all-to-all-start.2) | async-done | bytes 1048608 | tf_op jit(solution)/shard_map/all_to_all | solution.py:107
  227.8 63.7 %while.11 = (s32[]{:T(128)}, bf16[8,512,128]{2,1,0:T(8,128)(2,1)}, s32[8]{0:T(128)S(1)}, bf16[4096,128]{1,0:T(8,128)(2,1)}, bf16[4096,1,128]{2,0,1:T(8,128)(2,1)...) while((s32[]{:T(128)}, bf16[8,512,128]{2,1,0:T(8,128)(2,1)}, ...), condition=%wide.region_4.5_spmd.clone, body=%wide.region_1.4_spmd.clone.sunk | while | flops 1092681216 | bytes 27539636 | solution.py:82
  227.8 0.6 dynamic_slice.16
  229.0 2.6 fusion.46
  231.6 1.3 fusion.47
  232.9 2.8 fusion.48
  235.7 0.6 dynamic_slice.16
  237.0 2.6 fusion.46
  239.6 1.3 fusion.47
  240.9 2.8 fusion.48
  243.7 0.6 dynamic_slice.16
  245.0 2.6 fusion.46
  247.6 1.3 fusion.47
  248.8 2.8 fusion.48
  251.7 0.6 dynamic_slice.16
  252.9 2.6 fusion.46
  255.5 1.3 fusion.47
  256.8 2.8 fusion.48
  259.6 0.6 dynamic_slice.16
  260.9 2.6 fusion.46
  263.5 1.3 fusion.47
  264.8 2.8 fusion.48
  267.6 0.6 dynamic_slice.16
  268.9 2.6 fusion.46
  271.4 1.3 fusion.47
  272.7 2.8 fusion.48
  275.6 0.6 dynamic_slice.16
  276.8 2.6 fusion.46
  279.4 1.3 fusion.47
  280.7 2.8 fusion.48
  283.5 0.6 dynamic_slice.16
  284.8 2.6 fusion.46
  287.4 1.3 fusion.47
  288.7 2.8 fusion.48
  291.5 20.1 %all_to_all.67 = bf16[16,256,128]{2,1,0:T(8,128)(2,1)S(1)} all-to-all(bf16[16,256,128]{2,1,0:T(8,128)(2,1)} %bitcast.96), channel_id=1, replica_groups=mesh['section'=8,'seq'=16] {'seq'}, dimensions={0} | all-to-all | bytes 2097152 | tf_op jit(solution)/shard_map/all_to_all | solution.py:110
  311.5 0.5 copy.27
  312.1 1.5 collective-permute-start
  313.6 26.4 %collective-permute-done = bf16[256,2048]{0,1:T(8,128)(2,1)S(1)} collective-permute-done((bf16[256,2048]{0,1:T(8,128)(2,1)S(1)}, bf16[256,2048]{0,1:T(8,128)(2,1)S(1)}, u32[]{:S(2)}, u32[]{:S(2)}) %collective-permute-start) | collective-permute-done | bytes 1048608 | tf_op jit(solution)/shard_map/ppermute | solution.py:14
  340.1 1.4 copy.28
  (25 shorter events, 0.3 us)
Async XLA Ops:
  6.5 42.4 %all-gather.9.cloned.1.call-start = ((), (), s32[]{:S(2)}) async-start(), calls=%async_computation.5 | async-start | bytes 4456448 | tf_op jit(solution)/shard_map/all_gather | solution.py:94
  7.3 146.1 %all-gather.7.cloned.1.call-start = ((), (), s32[]{:S(2)}) async-start(), calls=%async_computation.4 | async-start | bytes 17825792 | tf_op jit(solution)/shard_map/all_gather | solution.py:93
  8.0 185.5 %all-gather.11.cloned.1.call-start = ((), (), s32[]{:S(2)}) async-start(), calls=%async_computation.6 | async-start | bytes 4456448 | tf_op jit(solution)/shard_map/all_gather | solution.py:95
  48.9 6.5 %copy-start = (bf16[1,256,4096]{2,1,0:T(8,128)(2,1)S(1)}, bf16[1,256,4096]{2,1,0:T(8,128)(2,1)}, u32[]{:S(2)}) copy-start(bf16[1,256,4096]{2,1,0:T(8,128)(2,1)} %param.7) | copy-start | bytes 6291460
  60.5 123.5 %all-to-all-start.1 = ((bf16[256,16,128]{2,0,1:T(8,128)(2,1)}), bf16[256,16,128]{2,0,1:T(8,128)(2,1)S(1)}, u32[]{:S(2)}, u32[]{:S(2)}) async-start(bf16[256,16,128]{2,0,1:T(8,128)(2,1)} %bitcast.12), calls=%async_computation.1 | async-start | bytes 2097152 | tf_op jit(solution)/shard_map/all_to_all | solution.py:106
  184.0 1.0 copy-start.1
  185.0 21.5 %all-to-all-start = ((bf16[256,16,128]{0,2,1:T(8,128)(2,1)}), bf16[256,16,128]{0,2,1:T(8,128)(2,1)S(1)}, u32[]{:S(2)}, u32[]{:S(2)}) async-start(bf16[256,16,128]{0,2,1:T(8,128)(2,1)} %pad_maximum_fusion), calls=%async_computation | async-start | bytes 2097152 | tf_op jit(solution)/shard_map/all_to_all | solution.py:105
  196.9 30.8 %copy-start.2 = (bf16[256,16,128]{2,0,1:T(8,128)(2,1)S(1)}, bf16[256,16,128]{2,0,1:T(8,128)(2,1)}, u32[]{:S(2)}) copy-start(bf16[256,16,128]{2,0,1:T(8,128)(2,1)} %copy-done.1) | copy-start | bytes 3145732
  207.6 20.2 %all-to-all-start.2 = ((bf16[256,16,128]{2,0,1:T(8,128)(2,1)}), bf16[256,16,128]{2,0,1:T(8,128)(2,1)S(1)}, u32[]{:S(2)}, u32[]{:S(2)}) async-start(bf16[256,16,128]{2,0,1:T(8,128)(2,1)} %bitcast.16), calls=%async_computation.2 | async-start | bytes 2097152 | tf_op jit(solution)/shard_map/all_to_all | solution.py:107
  312.1 28.0 %collective-permute-start = (bf16[256,2048]{0,1:T(8,128)(2,1)S(1)}, bf16[256,2048]{0,1:T(8,128)(2,1)S(1)}, u32[]{:S(2)}, u32[]{:S(2)}) collective-permute-start(bf16[256,2048]{0,1:T(8,128)(2,1)S(1)} %bitcast.97), channel_id=1, source_target_pairs={{112,0},{0,16},{16,32},{32,48},{48,64},{64,80},{80,96},{96,112},{1... | collective-permute-start | bytes 3145736 | tf_op jit(solution)/shard_map/ppermute | solution.py:14
Sparse Core Ops, SparseCore 0:
  9.0 39.8 all-gather.8
  50.6 102.7 all-gather.6
  155.1 38.3 all-gather.10
where the time goes:
time: 349 us; the launch traced here: 348 us
  waiting for transfers between devices  182 us (52%)
  matrix products  58.8 us (17%)
  local copies, waits for them, and re-layouts  39 us (11%)
  blocking collectives  20.1 us (6%)
  other arithmetic  14.9 us (4%)
  starting transfers between devices  14.5 us (4%)
  between operations  13.2 us (4%)
  loops' own time  5.19 us (1%)
    all_gather x1, waiting for transfers between devices, per_device(): lax.all_gather(query_weight, 'seq', axis=0, tiled=True)  88.7 us
    all_gather x1, waiting for transfers between devices, per_device(): lax.all_gather(key_weight, 'seq', axis=0, tiled=True)  37 us
    dot_general x2, local copies, waits for them, and re-layouts, per_device(): jnp.dot(normed, piece, preferred_element_type=jnp.float32)  27.3 us
    ppermute x1, waiting for transfers between devices, shifted(): return lax.ppermute(block, axis, route)  26.4 us
    dot_general x8, matrix products, one_block(): jnp.einsum('hqk,khd->qhd', probs, value_heads, preferred_element_type=jnp...  22.6 us
    dot_general x8, matrix products, one_block(): jnp.einsum('qhd,khd->hqk', query_block, key_heads, preferred_element_type...  20.7 us
    all_to_all x1, blocking collectives, per_device(): lax.all_to_all(attended, 'seq', split_axis=0, concat_axis=1, tiled=True)  20.1 us
    dot_general x3, matrix products, per_device(): jnp.dot(normed, piece, preferred_element_type=jnp.float32)  15.5 us
  transfers between devices with their start and end apart: 7, of which 6 were waited for; matrix products, arithmetic and copies ran while one was open for 14% of the time, Pallas kernels for 0%

commit v1 on v0

--- a/solution.py
+++ b/solution.py
@@ -6,6 +6,12 @@
 LOCAL_QUERY_HEADS = 16
 LOCAL_KEY_HEADS = 4
 HEAD_SIZE = 128
+
+
+def take_the_series_all(raw, link_axis):
+    return jnp.concatenate(
+        lax.all_to_all(jnp.stack(lax.psum(1, link_axis) * [raw], axis=0), link_axis, 0, 0), axis=0
+    )
 
 
 def shifted(block, axis, distance):
@@ -90,7 +96,7 @@
     key_weight = w_key[0]
     value_weight = w_value[0]
     pieces = (
-        lax.all_gather(query_weight, "seq", axis=0, tiled=True),
+        take_the_series_all(query_weight, "seq"),
         lax.all_gather(key_weight, "seq", axis=0, tiled=True),
         lax.all_gather(value_weight, "seq", axis=0, tiled=True),
     )

time: 349 us -> 476 us (1.36)
  waiting for transfers between devices: 182 us -> 271 us
  local copies, waits for them, and re-layouts: 39 us -> 68.3 us
  starting transfers between devices: 14.5 us -> 25.3 us
    all_gather x1, waiting for transfers between devices: 37 us -> 209 us  [per_device(): lax.all_gather(key_weight, 'seq', axis=0, tiled=True)]
    all_gather x1 -> x0, waiting for transfers between devices: 88.7 us -> none  [per_device(): lax.all_gather(query_weight, 'seq', axis=0, tiled=True)]
    all_to_all x0 -> x1, local copies, waits for them, and re-layouts: none -> 21.8 us  [take_the_series_all(): lax.all_to_all(jnp.stack(lax.psum(1, link_axis) * [raw], axis=0), link_ax...]
    another operation x0 -> x2, local copies, waits for them, and re-layouts: none -> 7.39 us  [the longest x1 5.91 us: take_the_series_all(): jnp.stack(lax.psum(1, link_axis) * [raw], axis=0)]
    all_to_all x0 -> x1, starting transfers between devices: none -> 6.72 us  [take_the_series_all(): lax.all_to_all(jnp.stack(lax.psum(1, link_axis) * [raw], axis=0), link_ax...]
    all_to_all x0 -> x1, waiting for transfers between devices: none -> 6.04 us  [take_the_series_all(): lax.all_to_all(jnp.stack(lax.psum(1, link_axis) * [raw], axis=0), link_ax...]
  transfers between devices with their start and end apart: 7 -> 7, of which waited for: 6 -> 5; matrix products, arithmetic and copies ran while one was open for 14% -> 15% of each run, Pallas kernels for 0% -> 0%
where the time goes in v1:
time: 476 us; the launch traced here: 474 us
  waiting for transfers between devices  271 us (57%)
  local copies, waits for them, and re-layouts  68.3 us (14%)
  matrix products  58.6 us (12%)
  starting transfers between devices  25.3 us (5%)
  blocking collectives  20.1 us (4%)
  between operations  13.6 us (3%)
  other arithmetic  12.6 us (3%)
  loops' own time  5.19 us (1%)
    all_gather x1, waiting for transfers between devices, per_device(): lax.all_gather(key_weight, 'seq', axis=0, tiled=True)  209 us
    dot_general x2, local copies, waits for them, and re-layouts, per_device(): jnp.dot(normed, piece, preferred_element_type=jnp.float32)  27.3 us
    ppermute x1, waiting for transfers between devices, shifted(): return lax.ppermute(block, axis, route)  26.4 us
    dot_general x8, matrix products, one_block(): jnp.einsum('hqk,khd->qhd', probs, value_heads, preferred_element_type=jnp...  22.6 us
    all_to_all x1, local copies, waits for them, and re-layouts, take_the_series_all(): lax.all_to_all(jnp.stack(lax.psum(1, link_axis) * [raw], axis=0), link_ax...  21.8 us
    dot_general x8, matrix products, one_block(): jnp.einsum('qhd,khd->hqk', query_block, key_heads, preferred_element_type...  20.7 us
    all_to_all x1, blocking collectives, per_device(): lax.all_to_all(attended, 'seq', split_axis=0, concat_axis=1, tiled=True)  20.1 us
    dot_general x3, matrix products, per_device(): jnp.dot(normed, piece, preferred_element_type=jnp.float32)  15.3 us
  transfers between devices with their start and end apart: 7, of which 5 were waited for; matrix products, arithmetic and copies ran while one was open for 15% of the time, Pallas kernels for 0%

profile of v1, /device:TPU:0, one launch (start us, length us, event | category | flops | bytes accessed | tf_op | source)
XLA Modules:
  0.0 474.2 jit_solution(3716623746996823905)
XLA Ops:
  6.5 1.5 copy.22
  8.0 5.9 %stack.3 = bf16[16,256,2048]{1,2,0:T(8,128)(2,1)} broadcast(bf16[256,2048]{0,1:T(8,128)(2,1)S(1)} %copy.22), dimensions={1,2} | broadcast | bytes 17825792 | tf_op jit(solution)/shard_map/stack | solution.py:13
  13.9 6.7 %all-to-all-start = ((bf16[16,256,2048]{1,2,0:T(8,128)(2,1)}), bf16[16,256,2048]{1,2,0:T(8,128)(2,1)}, u32[]{:S(2)}, u32[]{:S(2)}) async-start(bf16[16,256,2048]{1,2,0:T(8,128)(2,1)} %stack.3), calls=%async_computation | async-start | bytes 33554432 | tf_op jit(solution)/shard_map/all_to_all | solution.py:13
  20.7 0.7 all-gather.5.cloned.1.call-update
  21.4 0.7 all-gather.7.cloned.1.call-update
  22.2 0.5 fusion.13
  22.7 0.3 multiply_cosine_fusion
  23.1 208.7 %all-gather.5.cloned.1.call-done = bf16[1,4096,512]{2,1,0:T(8,128)(2,1)} async-done(((bf16[1,256,512]{2,1,0:T(8,128)(2,1)}), bf16[1,4096,512]{2,1,0:T(8,128)(2,1)}) %all-gather.5.cloned.1.call-update) | async-done | bytes 4194320 | tf_op jit(solution)/shard_map/all_gather | solution.py:100
  231.8 6.4 %copy.26 = bf16[512,4096]{1,0:T(8,128)(2,1)} copy(bf16[512,4096]{0,1:T(8,128)(2,1)} %bitcast.90) | data formatting | bytes 8388608 | tf_op jit(solution)/shard_map/dot_general | solution.py:104
  238.2 3.5 fusion.34
  242.0 6.0 %all-to-all-done = bf16[16,256,2048]{1,2,0:T(8,128)(2,1)} async-done(((bf16[16,256,2048]{1,2,0:T(8,128)(2,1)}), bf16[16,256,2048]{1,2,0:T(8,128)(2,1)}, u32[]{:S(2)}, u32[]{:S(2)}) %all-to-all-start) | async-done | bytes 16777248 | tf_op jit(solution)/shard_map/all_to_all | solution.py:13
  248.1 1.2 broadcast_in_dim.17
  249.3 7.4 %all-to-all-start.2 = ((bf16[256,16,128]{2,0,1:T(8,128)(2,1)}), bf16[256,16,128]{2,0,1:T(8,128)(2,1)S(1)}, u32[]{:S(2)}, u32[]{:S(2)}) async-start(bf16[256,16,128]{2,0,1:T(8,128)(2,1)} %bitcast.13), calls=%async_computation.2 | async-start | bytes 2097152 | tf_op jit(solution)/shard_map/all_to_all | solution.py:112
  256.7 21.8 %copy.23 = bf16[16,256,2048]{2,1,0:T(8,128)(2,1)} copy(bf16[16,256,2048]{1,2,0:T(8,128)(2,1)} %all-to-all-done) | data formatting | bytes 33554432 | tf_op jit(solution)/shard_map/all_to_all | solution.py:13
  278.5 20.9 %copy.24 = bf16[2048,4096]{1,0:T(8,128)(2,1)} copy(bf16[2048,4096]{0,1:T(8,128)(2,1)} %bitcast.88) | data formatting | bytes 33554432 | tf_op jit(solution)/shard_map/dot_general | solution.py:104
  299.4 8.3 %fusion.36 = f32[256,16,128]{0,2,1:T(8,128)S(1)} fusion(bf16[16,128,4096]{2,1,0:T(8,128)(2,1)} %bitcast.89, bf16[1,256,4096]{2,1,0:T(8,128)(2,1)S(1)} %copy-done, f32[4096]{0:T(1024)S(1)} %bitcast.102, f32[256]{0:T(256)S(1)} %add_rsqrt_fusion), kind=kOutput, calls=%fused_computation.35 | convolution fusion | flops 4299161600 | bytes 20988928 | tf_op jit(solution)/shard_map/dot_general | solution.py:104
  307.7 0.3 subtract_convert_fusion
  308.1 1.0 pad_maximum_fusion
  309.1 1.0 copy-done.1
  310.1 5.7 %all-to-all-start.1 = ((bf16[256,16,128]{0,2,1:T(8,128)(2,1)}), bf16[256,16,128]{0,2,1:T(8,128)(2,1)S(1)}, u32[]{:S(2)}, u32[]{:S(2)}) async-start(bf16[256,16,128]{0,2,1:T(8,128)(2,1)} %pad_maximum_fusion), calls=%async_computation.1 | async-start | bytes 2097152 | tf_op jit(solution)/shard_map/all_to_all | solution.py:111
  315.8 3.5 fusion.29
  319.3 13.0 %all-to-all-done.1 = bf16[256,16,128]{0,2,1:T(8,128)(2,1)S(1)} async-done(((bf16[256,16,128]{0,2,1:T(8,128)(2,1)}), bf16[256,16,128]{0,2,1:T(8,128)(2,1)S(1)}, u32[]{:S(2)}, u32[]{:S(2)}) %all-to-all-start.1) | async-done | bytes 1048608 | tf_op jit(solution)/shard_map/all_to_all | solution.py:111
  332.3 1.2 broadcast_in_dim.19
  333.5 3.8 all-to-all-start.3
  337.3 1.3 copy.25
  338.6 15.0 %all-to-all-done.3 = bf16[256,16,128]{2,0,1:T(8,128)(2,1)S(1)} async-done(((bf16[256,16,128]{2,0,1:T(8,128)(2,1)}), bf16[256,16,128]{2,0,1:T(8,128)(2,1)S(1)}, u32[]{:S(2)}, u32[]{:S(2)}) %all-to-all-start.3) | async-done | bytes 1048608 | tf_op jit(solution)/shard_map/all_to_all | solution.py:113
  353.6 63.7 %while.11 = (s32[]{:T(128)}, bf16[8,512,128]{2,1,0:T(8,128)(2,1)}, s32[8]{0:T(128)S(1)}, bf16[4096,128]{1,0:T(8,128)(2,1)}, bf16[4096,1,128]{2,0,1:T(8,128)(2,1)...) while((s32[]{:T(128)}, bf16[8,512,128]{2,1,0:T(8,128)(2,1)}, ...), condition=%wide.region_4.5_spmd.clone, body=%wide.region_1.4_spmd.clone.sunk | while | flops 1092681216 | bytes 27540136 | solution.py:88
  353.6 0.6 dynamic_slice.16
  354.9 2.6 fusion.46
  357.5 1.3 fusion.47
  358.8 2.8 fusion.48
  361.6 0.6 dynamic_slice.16
  362.9 2.6 fusion.46
  365.5 1.3 fusion.47
  366.7 2.8 fusion.48
  369.6 0.6 dynamic_slice.16
  370.8 2.6 fusion.46
  373.4 1.3 fusion.47
  374.7 2.8 fusion.48
  377.5 0.6 dynamic_slice.16
  378.8 2.6 fusion.46
  381.4 1.3 fusion.47
  382.7 2.8 fusion.48
  385.5 0.6 dynamic_slice.16
  386.8 2.6 fusion.46
  389.4 1.3 fusion.47
  390.6 2.8 fusion.48
  393.5 0.6 dynamic_slice.16
  394.7 2.6 fusion.46
  397.3 1.3 fusion.47
  398.6 2.8 fusion.48
  401.4 0.6 dynamic_slice.16
  402.7 2.6 fusion.46
  405.3 1.3 fusion.47
  406.6 2.8 fusion.48
  409.4 0.6 dynamic_slice.16
  410.7 2.6 fusion.46
  413.2 1.3 fusion.47
  414.5 2.8 fusion.48
  417.4 20.1 %all_to_all.72 = bf16[16,256,128]{2,1,0:T(8,128)(2,1)S(1)} all-to-all(bf16[16,256,128]{2,1,0:T(8,128)(2,1)} %bitcast.98), channel_id=1, replica_groups=mesh['section'=8,'seq'=16] {'seq'}, dimensions={0} | all-to-all | bytes 2097152 | tf_op jit(solution)/shard_map/all_to_all | solution.py:116
  437.4 0.5 copy.29
  437.9 1.6 collective-permute-start
  439.5 26.4 %collective-permute-done = bf16[256,2048]{0,1:T(8,128)(2,1)S(1)} collective-permute-done((bf16[256,2048]{0,1:T(8,128)(2,1)S(1)}, bf16[256,2048]{0,1:T(8,128)(2,1)S(1)}, u32[]{:S(2)}, u32[]{:S(2)}) %collective-permute-start) | collective-permute-done | bytes 1048608 | tf_op jit(solution)/shard_map/ppermute | solution.py:20
  465.9 1.4 copy.30
  (29 shorter events, 0.5 us)
Async XLA Ops:
  13.9 8.2 %copy-start.3 = (bf16[1,4096]{1,0:T(2,128)(2,1)S(1)}, bf16[1,4096]{1,0:T(2,128)(2,1)}, u32[]{:S(2)}) copy-start(bf16[1,4096]{1,0:T(2,128)(2,1)} %param.8) | copy-start | bytes 24580
  13.9 8.3 %copy-start = (bf16[1,256,4096]{2,1,0:T(8,128)(2,1)S(1)}, bf16[1,256,4096]{2,1,0:T(8,128)(2,1)}, u32[]{:S(2)}) copy-start(bf16[1,256,4096]{2,1,0:T(8,128)(2,1)} %param.7) | copy-start | bytes 6291460
  13.9 234.1 %all-to-all-start = ((bf16[16,256,2048]{1,2,0:T(8,128)(2,1)}), bf16[16,256,2048]{1,2,0:T(8,128)(2,1)}, u32[]{:S(2)}, u32[]{:S(2)}) async-start(bf16[16,256,2048]{1,2,0:T(8,128)(2,1)} %stack.3), calls=%async_computation | async-start | bytes 33554432 | tf_op jit(solution)/shard_map/all_to_all | solution.py:13
  20.7 211.1 %all-gather.5.cloned.1.call-start = ((), (), s32[]{:S(2)}) async-start(), calls=%async_computation.5 | async-start | bytes 4456448 | tf_op jit(solution)/shard_map/all_gather | solution.py:100
  21.4 294.4 %all-gather.7.cloned.1.call-start = ((), (), s32[]{:S(2)}) async-start(), calls=%async_computation.6 | async-start | bytes 4456448 | tf_op jit(solution)/shard_map/all_gather | solution.py:101
  249.3 59.8 %all-to-all-start.2 = ((bf16[256,16,128]{2,0,1:T(8,128)(2,1)}), bf16[256,16,128]{2,0,1:T(8,128)(2,1)S(1)}, u32[]{:S(2)}, u32[]{:S(2)}) async-start(bf16[256,16,128]{2,0,1:T(8,128)(2,1)} %bitcast.13), calls=%async_computation.2 | async-start | bytes 2097152 | tf_op jit(solution)/shard_map/all_to_all | solution.py:112
  309.1 1.0 copy-start.1
  310.1 22.2 %all-to-all-start.1 = ((bf16[256,16,128]{0,2,1:T(8,128)(2,1)}), bf16[256,16,128]{0,2,1:T(8,128)(2,1)S(1)}, u32[]{:S(2)}, u32[]{:S(2)}) async-start(bf16[256,16,128]{0,2,1:T(8,128)(2,1)} %pad_maximum_fusion), calls=%async_computation.1 | async-start | bytes 2097152 | tf_op jit(solution)/shard_map/all_to_all | solution.py:111
  319.3 34.4 %copy-start.2 = (bf16[256,16,128]{2,0,1:T(8,128)(2,1)S(1)}, bf16[256,16,128]{2,0,1:T(8,128)(2,1)}, u32[]{:S(2)}) copy-start(bf16[256,16,128]{2,0,1:T(8,128)(2,1)} %copy-done.1) | copy-start | bytes 3145732
  333.5 20.2 %all-to-all-start.3 = ((bf16[256,16,128]{2,0,1:T(8,128)(2,1)}), bf16[256,16,128]{2,0,1:T(8,128)(2,1)S(1)}, u32[]{:S(2)}, u32[]{:S(2)}) async-start(bf16[256,16,128]{2,0,1:T(8,128)(2,1)} %bitcast.17), calls=%async_computation.3 | async-start | bytes 2097152 | tf_op jit(solution)/shard_map/all_to_all | solution.py:113
  437.9 28.0 %collective-permute-start = (bf16[256,2048]{0,1:T(8,128)(2,1)S(1)}, bf16[256,2048]{0,1:T(8,128)(2,1)S(1)}, u32[]{:S(2)}, u32[]{:S(2)}) collective-permute-start(bf16[256,2048]{0,1:T(8,128)(2,1)S(1)} %bitcast.99), channel_id=1, source_target_pairs={{112,0},{0,16},{16,32},{32,48},{48,64},{64,80},{80,96},{96,112},{1... | collective-permute-start | bytes 3145736 | tf_op jit(solution)/shard_map/ppermute | solution.py:20
Sparse Core Ops, SparseCore 0:
  23.2 208.5 all-gather.4
  233.5 56.7 all-gather.6
